TPU v7x, 32 devices: a whole 2x2x4 slice. The times are simulated.
32 devices in a mesh: grp: 2 (over x), slab: 16 (over z, y, core).
Axes of the slice: x: 2, y: 2, z: 4, core: 2. Of those that a mesh axis runs over, the one named last changes fastest.
Arguments:
- volume: bfloat16 [64, 1024, 1024], P(('grp', 'slab')), parts along dimension 0, may hold values from -60 to 60
- plane_shift: int32 [4, 32], P('grp', 'slab'), parts along dimension 0, may hold values from -64 to 64
- plane_weight: float32 [4, 32], P('grp', 'slab'), parts along dimension 0, may hold values from 0 to 1
- column_left: int32 [4, 1024], P('grp'), parts along dimension 0, may hold values from 0 to 1022
- column_weight: float32 [4, 1024], P('grp'), parts along dimension 0, may hold values from 0 to 1
- window_center: int32 [4, 2], P('grp'), parts along dimension 0, may hold values from -200 to 199
- tilt_owner: int32 [32], P('grp'), parts along dimension 0, may hold values from 0 to 15, each once
- reference_band: float32 [32, 2, 128, 128], P(('grp', 'slab')), parts along dimension 0, may hold values from -6 to 6
Outputs:
- correlation: float32 [4, 16, 128], P('grp', 'slab'), parts along dimension 0
- peaks: float32 [4], P('grp'), parts along dimension 0
There are 2 independent parts, one for each index of `grp`. A program takes and returns all parts, laid end to end along the dimension named above; each array names one. Nothing has to cross between parts.
Inputs may be any that keep to these rules, and one draw needn't show every extreme that they name: `tilt_owner`: the first 2 entries name the owners of the tilts, one slab index each.
All inputs are finite; a program needn't handle non-finite values.
Results may differ from a plain program's by a relative error of at most 0.0003.
Values sent between devices are 32-bit elements; how exact they have to be, the bound alone decides.
A program may use at most 128 MiB of HBM per device.

v0:
```python
import functools
import math

import jax
import jax.numpy as jnp
import numpy as np
from jax import lax
from jax.experimental import pallas as pl
from jax.experimental.pallas import tpu as pltpu
from jax.sharding import PartitionSpec as P

MESH = pl.DeviceIdType.MESH
LANES = 128
CHUNK = 256
BF16 = jnp.bfloat16
F32 = jnp.float32


def phases(left, right, length):
    angle = (np.outer(left, right) % length) * (2.0 * math.pi / length)
    return np.cos(angle), np.sin(angle)


def split(values):
    high = values.astype(np.float32).astype(BF16)
    low = (values - high.astype(np.float64)).astype(np.float32).astype(BF16)
    return high, low


def halves(value):
    high = value.astype(BF16)
    return high, (value - high.astype(F32)).astype(BF16)


def row_table(length, band):
    count = band // 2 + 8
    cos, sin = phases(np.arange(count), np.arange(length), length)
    return np.concatenate(split(np.concatenate([cos, sin])))


def col_table(length, band):
    cos, sin = phases(np.arange(length), np.arange(band), length)
    return np.stack(split(np.concatenate([cos, sin], axis=1)))


def window_table(length, band, columns):
    cos, sin = phases(np.arange(band), np.arange(columns), length)
    return np.concatenate([cos, sin], axis=1).astype(np.float32)


def fused_kernel(
    n, center_ref, owner_ref, shift_ref, weight_ref, left_ref, share_ref, mine_ref, window_ref,
    volume_ref, rowt_ref, colt_ref, out_ref,
    vol, rowt, colt, onehot, rows, rolled, summed, stack, proj, sems,
    ref_out, ref_in, spec_out, spec_in, part_out, part_in, peak_out, peak_in,
    ref_send, ref_recv, spec_send, spec_recv, part_send, part_recv, peak_send, peak_recv,
):
    me = lax.axis_index("slab")
    planes, height, width = volume_ref.shape
    tilts = left_ref.shape[0]
    blocks = width // LANES
    chunks = width // CHUNK
    count = rows.shape[2]

    table = pltpu.make_async_copy(rowt_ref, rowt, sems.at[0])
    table.start()
    loads = []
    for z in range(planes):
        for c in range(chunks):
            part = (z, slice(None), pl.ds(c * CHUNK, CHUNK))
            load = pltpu.make_async_copy(volume_ref.at[part], vol.at[part], sems.at[2 + z * chunks + c])
            load.start()
            loads.append(load)
    last_table = pltpu.make_async_copy(colt_ref, colt, sems.at[1])
    last_table.start()

    band = mine_ref.shape[-1]
    length = width
    half = band // 2
    sines = count // 2
    per = max(1, half // n)
    owners = half // per
    win_cols = out_ref.shape[-1]

    def on_owner(device, body):
        if owners == n:
            body()
        else:
            pl.when(device < owners)(body)

    barrier = pltpu.get_barrier_semaphore()
    for k in range(1, n):
        pl.semaphore_signal(
            barrier, inc=1, device_id={"slab": lax.rem(me + k, n)}, device_id_type=MESH
        )

    def sending(source, into, send, recv, k):
        return pltpu.make_async_remote_copy(
            src_ref=source,
            dst_ref=into.at[me],
            send_sem=send.at[k],
            recv_sem=recv.at[k],
            device_id={"slab": lax.rem(me + k, n)},
            device_id_type=MESH,
        )

    def arriving(into, send, recv, k):
        source = lax.rem(me + n - k, n)
        return pltpu.make_async_remote_copy(
            src_ref=into.at[source],
            dst_ref=into.at[source],
            send_sem=send.at[k],
            recv_sem=recv.at[k],
            device_id={"slab": source},
            device_id_type=MESH,
        )

    def scatter(out, into, send, recv, k):
        return sending(out.at[lax.rem(me + k, n)], into, send, recv, k)

    def scatter_all(*group):
        for k in range(1, n):
            on_owner(lax.rem(me + k, n), lambda: scatter(*group, k).start())

    refs = (ref_out, ref_in, ref_send, ref_recv)
    spectra = [
        (spec_out.at[t], spec_in.at[t], spec_send.at[t], spec_recv.at[t]) for t in range(tilts)
    ]

    for e in range(owners):
        for part in range(2):
            base = part * 2 * per
            first = half + e * per
            ref_out[e, base : base + per, :] = mine_ref[0, part, first : first + per, :]
            for k in range(per):
                row = (half - e * per - k) if e * per + k else 0
                ref_out[e, base + per + k : base + per + k + 1, :] = mine_ref[0, part, row : row + 1, :]

    @pl.loop(0, blocks)
    def _(b):
        first = pl.multiple_of(b * LANES, LANES)
        ids = lax.broadcasted_iota(jnp.int32, (LANES, width), 0) + first
        for t in range(tilts):
            hit = jnp.where(ids == left_ref[t : t + 1, :], 1.0, 0.0)
            onehot[t, pl.ds(first, LANES), :] = hit.astype(BF16)

    table.wait()
    for z in range(planes):
        for c in range(chunks):
            loads[z * chunks + c].wait()
            out = jnp.dot(
                rowt[...], vol[z, :, c * CHUNK : (c + 1) * CHUNK], preferred_element_type=F32
            )
            out = out[:count] + out[count:]
            for b in range(CHUNK // LANES):
                rows[z, c * (CHUNK // LANES) + b] = out[:, b * LANES : (b + 1) * LANES]
        if z == 0:
            pl.semaphore_wait(barrier, n - 1)
            scatter_all(*refs)

    lane = lax.broadcasted_iota(jnp.int32, (count, LANES), 1)
    zero = jnp.zeros((count, LANES), F32)
    top = lax.broadcasted_iota(jnp.int32, (half, band), 0) == 0
    for t in range(tilts):
        terms = []
        for z in range(planes):
            for extra in range(2):
                slot = z * 2 + extra
                shift = shift_ref[t, z] + extra
                turn = shift & (LANES - 1)
                jump = jnp.where(shift < 0, 1, 0)
                weight = weight_ref[t, z] if extra else 1.0 - weight_ref[t, z]
                rolled[slot, 0] = zero
                rolled[slot, blocks + 1] = zero
                for b in range(blocks):
                    rolled[slot, b + 1] = pltpu.roll(rows[z, b] * weight, turn, 1)
                terms.append((slot, lane >= turn, jump))
        for b in range(blocks):
            total = None
            for slot, mask, jump in terms:
                term = jnp.where(mask, rolled[slot, b + 1 + jump], rolled[slot, b + jump])
                total = term if total is None else total + term
            summed[b] = total
            high, low = halves(total)
            here = slice(b * LANES, (b + 1) * LANES)
            stack[0, :, here] = high
            stack[1, :, here] = low
        for b in range(blocks):
            ahead = summed[(b + 1) % blocks]
            right = pltpu.roll(jnp.where(lane == 0, ahead, summed[b]), LANES - 1, 1)
            high, low = halves(right)
            here = slice(b * LANES, (b + 1) * LANES)
            stack[2, :, here] = high
            stack[3, :, here] = low
        for c in range(chunks):
            here = slice(c * CHUNK, (c + 1) * CHUNK)
            picked = jnp.dot(
                stack[...].reshape(4 * count, width), onehot[t, :, here], preferred_element_type=F32
            )
            share = share_ref[t : t + 1, here]
            value = (1.0 - share) * (picked[:count] + picked[count : 2 * count])
            value = value + share * (picked[2 * count : 3 * count] + picked[3 * count :])
            high, low = halves(value)
            proj[0, :, here] = high
            proj[1, :, here] = low
        if t == 0:
            last_table.wait()
        both = jnp.dot(
            proj[...].reshape(2 * count, width), colt[0], preferred_element_type=F32
        )
        rest = jnp.dot(proj[0], colt[1], preferred_element_type=F32)
        partial = both[:count] + both[count:] + rest
        cos_cos = partial[:sines, :band]
        cos_sin = partial[:sines, band:]
        sin_cos = partial[sines:, :band]
        sin_sin = partial[sines:, band:]
        low_re = cos_cos + sin_sin
        low_im = sin_cos - cos_sin
        kinds = (
            (cos_cos - sin_sin)[:half],
            jnp.where(top, low_re[half : half + 1], low_re[:half]),
            -(sin_cos + cos_sin)[:half],
            jnp.where(top, low_im[half : half + 1], low_im[:half]),
        )
        for kind, value in enumerate(kinds):
            base = kind * per
            for e in range(owners):
                spec_out[t, e, base : base + per, :] = value[e * per : (e + 1) * per]
        scatter_all(*spectra[t])

    def wave(ints):
        angle = (ints & (length - 1)).astype(F32) * (2.0 * math.pi / length)
        return jnp.cos(angle), jnp.sin(angle)

    freq = lax.broadcasted_iota(jnp.int32, (2 * per, band), 1)
    slot = lax.broadcasted_iota(jnp.int32, (n, 2 * per), 1)
    step = lax.broadcasted_iota(jnp.int32, (n, 2 * per), 0) - n // 2
    lower = slot >= per
    place = me * per + jnp.where(lower, slot - per, slot)
    freq_row = jnp.where(lower, jnp.where(place == 0, -half, -place), place)
    col_waves = [wave(freq * (center_ref[t, 1] - win_cols // 2)) for t in range(tilts)]
    row_waves = [wave(freq_row * (center_ref[t, 0] + step)) for t in range(tilts)]
    spot = lax.broadcasted_iota(jnp.int32, (1, win_cols), 1)

    def contribute():
        ref_in[me] = ref_out[me]
        for k in range(1, n):
            arriving(*refs[1:], k).wait_recv()
        real_parts, imag_parts = [], []
        energy = jnp.zeros((1, win_cols), F32)
        for t in range(tilts):
            spec_in[t, me] = spec_out[t, me]
            for k in range(1, n):
                arriving(*spectra[t][1:], k).wait_recv()
            total = spec_in[t, 0]
            for e in range(1, n):
                total = total + spec_in[t, e]
            spec_re, spec_im = total[: 2 * per], total[2 * per :]
            owned = ref_in[owner_ref[t]]
            ref_re, ref_im = owned[: 2 * per], owned[2 * per :]
            cross_re = spec_re * ref_re + spec_im * ref_im
            cross_im = spec_im * ref_re - spec_re * ref_im
            cos, sin = col_waves[t]
            real_parts.append(cross_re * cos - cross_im * sin)
            imag_parts.append(cross_re * sin + cross_im * cos)
            for kind, (real, imag) in enumerate(((spec_re, spec_im), (ref_re, ref_im))):
                power = jnp.sum(real * real + imag * imag, axis=0, keepdims=True)
                power = jnp.sum(power, axis=1, keepdims=True)
                energy = jnp.where(spot == kind * tilts + t, power, energy)
        turned = jnp.dot(
            jnp.concatenate(real_parts + imag_parts, axis=0), window_ref[...],
            precision=lax.Precision.HIGHEST, preferred_element_type=F32,
        )
        mid = tilts * 2 * per
        moved_re = turned[:mid, :win_cols] - turned[mid:, win_cols:]
        moved_im = turned[:mid, win_cols:] + turned[mid:, :win_cols]
        for t in range(tilts):
            here = slice(t * 2 * per, (t + 1) * 2 * per)
            cos, sin = row_waves[t]
            left = jnp.concatenate([cos, -sin], axis=1)
            right = jnp.concatenate([moved_re[here], moved_im[here]], axis=0)
            value = jnp.dot(
                left, right, precision=lax.Precision.HIGHEST, preferred_element_type=F32
            )
            for i in range(n):
                part_out[i, t : t + 1, :] = value[i : i + 1]
        for i in range(n):
            part_out[i, tilts : tilts + 1, :] = energy
        for k in range(1, n):
            scatter(part_out, part_in, part_send, part_recv, k).start()
        part_in[me] = part_out[me]

    on_owner(me, contribute)

    for k in range(1, n):
        source = lax.rem(me + n - k, n)
        on_owner(source, lambda: arriving(part_in, part_send, part_recv, k).wait_recv())
    total = part_in[0]
    for e in range(1, owners):
        total = total + part_in[e]
    means = total[tilts : tilts + 1] / (band * band) + 1e-06
    lines = []
    for t in range(tilts):
        scale = band * jnp.sqrt(means[:, t : t + 1] * means[:, tilts + t : tilts + t + 1])
        lines.append(total[t : t + 1] / scale)
    line = jnp.concatenate(lines, axis=0)
    peak_out[...] = line
    for k in range(1, n):
        sending(peak_out, peak_in, peak_send, peak_recv, k).start()
    peak_in[me] = line
    out_ref[0] = line
    for group in [refs] + spectra:
        for k in range(1, n):
            on_owner(lax.rem(me + k, n), lambda: scatter(*group, k).wait_send())

    def drain():
        for k in range(1, n):
            scatter(part_out, part_in, part_send, part_recv, k).wait_send()

    on_owner(me, drain)
    for k in range(1, n):
        arriving(peak_in, peak_send, peak_recv, k).wait_recv()
    best = peak_in[0]
    for e in range(1, n):
        best = jnp.maximum(best, peak_in[e])
    out_ref[1] = best
    for k in range(1, n):
        sending(peak_out, peak_in, peak_send, peak_recv, k).wait_send()


def finish_kernel(both_ref, corr_ref, peak_ref):
    for t in range(both_ref.shape[1]):
        corr_ref[t] = both_ref[0, t : t + 1, :]
        peak_ref[t] = jnp.max(both_ref[1, t : t + 1, :])


def run(n, volume, shift, weight, left, share, center, owner, mine):
    planes, height, width = volume.shape
    tilts = left.shape[0]
    band = mine.shape[-1]
    win_cols = band
    rowt = row_table(height, band)
    colt = col_table(width, band)
    window = window_table(width, band, win_cols)
    count = rowt.shape[0] // 2
    blocks = width // LANES
    per = max(1, band // 2 // n)
    owners = band // 2 // per
    smem = pl.BlockSpec(memory_space=pltpu.SMEM)
    vmem = pl.BlockSpec(memory_space=pltpu.VMEM)
    hbm = pl.BlockSpec(memory_space=pl.ANY)
    dma = pltpu.SemaphoreType.DMA
    both = pl.pallas_call(
        functools.partial(fused_kernel, n),
        out_shape=jax.ShapeDtypeStruct((2, tilts, win_cols), F32),
        in_specs=[smem] * 4 + [vmem] * 4 + [hbm] * 3,
        out_specs=vmem,
        scratch_shapes=[
            pltpu.VMEM((planes, height, width), BF16),
            pltpu.VMEM(rowt.shape, BF16),
            pltpu.VMEM(colt.shape, BF16),
            pltpu.VMEM((tilts, width, width), BF16),
            pltpu.VMEM((planes, blocks, count, LANES), F32),
            pltpu.VMEM((planes * 2, blocks + 2, count, LANES), F32),
            pltpu.VMEM((blocks, count, LANES), F32),
            pltpu.VMEM((4, count, width), BF16),
            pltpu.VMEM((2, count, width), BF16),
            dma((2 + planes * (width // CHUNK),)),
            pltpu.VMEM((owners, 4 * per, band), F32),
            pltpu.VMEM((n, 4 * per, band), F32),
            pltpu.VMEM((tilts, owners, 4 * per, band), F32),
            pltpu.VMEM((tilts, n, 4 * per, band), F32),
            pltpu.VMEM((n, tilts + 1, win_cols), F32),
            pltpu.VMEM((n, tilts + 1, win_cols), F32),
            pltpu.VMEM((tilts, win_cols), F32),
            pltpu.VMEM((n, tilts, win_cols), F32),
            dma((n,)), dma((n,)), dma((tilts, n)), dma((tilts, n)),
            dma((n,)), dma((n,)), dma((n,)), dma((n,)),
        ],
        compiler_params=pltpu.CompilerParams(
            collective_id=0, has_side_effects=True, vmem_limit_bytes=56 * 1024 * 1024
        ),
        name="fused",
    )(
        center, owner, shift, weight, left, share, mine, jnp.asarray(window),
        volume, jnp.asarray(rowt), jnp.asarray(colt),
    )
    return pl.pallas_call(
        finish_kernel,
        out_shape=(
            jax.ShapeDtypeStruct((tilts, 1, win_cols), F32),
            jax.ShapeDtypeStruct((tilts,), F32),
        ),
        in_specs=[vmem],
        out_specs=(vmem, smem),
        name="finish",
    )(both)


def solution(mesh):
    n = mesh.shape["slab"]

    def per_device(volume, shift, weight, left, share, center, owner, bands):
        return run(n, volume, shift, weight, left, share, center, owner, bands)

    placed = (
        P(("grp", "slab"), None, None),
        P("grp", "slab"),
        P("grp", "slab"),
        P("grp", None),
        P("grp", None),
        P("grp", None),
        P("grp"),
        P(("grp", "slab"), None, None, None),
    )
    return jax.shard_map(
        per_device,
        mesh=mesh,
        in_specs=placed,
        out_specs=(P("grp", "slab", None), P("grp")),
        check_vma=False,
    )
```

profile of v0, /device:TPU:0, one launch (start us, length us, event | category | flops | bytes accessed | tf_op | source)
XLA Modules:
  0.0 32.0 jit_solution(7820746667278908658)
XLA Ops:
  0.6 30.0 %fused.1.both_ref = f32[2,2,128]{2,1,0:T(2,128)} custom-call(s32[2,2]{1,0:T(2,128)} %center_ref.1, s32[16]{0:T(128)} %owner_ref.1, s32[2,2]{1,0:T(2,128)} %shift_ref.1, f32[2,2]{1,0:T(2,128)} %weight_ref.1, s32[2,1024]{1,0:T(2,128)} %left_ref.1, f32[2,1024]{1,0:T(2,128)} %share_ref.1, f32[1,2,128,128]{3,2,1,0:T(8,128)} %mine_ref.1, ...), custom_call_target="tpu_custom_call" | custom-call | tf_op jit(solution)/shard_map/fused/pallas_call | solution.py:353
  30.7 1.3 %finish.1 = (f32[2,1,128]{2,1,0:T(1,128)}, f32[2]{0:T(128)}) custom-call(f32[2,2,128]{2,1,0:T(2,128)} %fused.1.both_ref), custom_call_target="tpu_custom_call" | custom-call | tf_op jit(solution)/shard_map/finish/pallas_call | solution.py:388
where the time goes:
time: 32.1 us; the launch traced here: 32 us
  Pallas kernels  31.4 us (98%)
  between operations  0.64 us (2%)
    pallas_call x1, Pallas kernels, run(): pl.pallas_call(functools.partial(fused_kernel, n), out_shape=jax.ShapeDty...  30 us
    pallas_call x1, Pallas kernels, run(): pl.pallas_call(finish_kernel, out_shape=(jax.ShapeDtypeStruct((tilts, 1,...  1.32 us

commit v1 on v0

v1 whole, which is shorter than its diff:
```python
import functools
import math

import jax
import jax.numpy as jnp
import numpy as np
from jax import lax
from jax.experimental import pallas as pl
from jax.experimental.pallas import tpu as pltpu
from jax.sharding import PartitionSpec as P

MESH = pl.DeviceIdType.MESH
LANES = 128
SUBLANES = 8
CHUNK = 256
OWNERS = 4
BF16 = jnp.bfloat16
F32 = jnp.float32


def phases(left, right, length):
    angle = (np.outer(left, right) % length) * (2.0 * math.pi / length)
    return np.cos(angle), np.sin(angle)


def split(values):
    high = values.astype(np.float32).astype(BF16)
    low = (values - high.astype(np.float64)).astype(np.float32).astype(BF16)
    return high, low


def halves(value):
    high = value.astype(BF16)
    return high, (value - high.astype(F32)).astype(BF16)


def row_table(length, band):
    half = band // 2
    cos, sin = phases(np.arange(half + 1), np.arange(length), length)
    last = np.zeros((SUBLANES, length))
    last[0] = sin[half]
    return np.concatenate(split(np.concatenate([cos[:half], cos[half:], sin[1:half], last])))


def col_table(length, band, owners):
    cos, sin = phases(np.arange(band), np.arange(length), length)
    own = band // owners
    rows = []
    for w in range(owners):
        rows += [cos[w * own : (w + 1) * own], sin[w * own : (w + 1) * own]]
    return np.concatenate(split(np.concatenate(rows)))


def fused_kernel(
    n, owners, center_hbm, owner_hbm, shift_hbm, weight_hbm,
    left_ref, share_ref, mine_ref, volume_ref, rowt_ref, colt_ref, corr_ref, peak_ref,
    center_ref, owner_ref, shift_ref, weight_ref, left, share, mine, vol, rowt, colt, onehot, shares, rows, extra, line, summed, stack, proj,
    perm, ref_out, ref_in, spec_out, spec_sib, spec_in, part_out, part_in,
    sems, ref_send, ref_recv, sib_send, sib_recv, spec_send, spec_recv, part_send, part_recv,
):
    me = lax.axis_index("slab")
    core = lax.rem(me, 2)
    sibling = me + 1 - 2 * core
    chip = me // 2
    planes, height, width = volume_ref.shape
    tilts = left_ref.shape[0]
    band = mine_ref.shape[-1]
    half = band // 2
    own = band // owners
    blocks = width // LANES
    chunks = width // CHUNK
    count = rowt_ref.shape[0] // 2
    pad = (rows.shape[1] - width) // 2
    length = width
    win_cols = corr_ref.shape[-1]
    first, stride = n // owners + 1, max(2, n // (2 * owners))
    places = [first + w * stride for w in range(owners)]

    def local(source, into, k):
        copy = pltpu.make_async_copy(source, into, sems.at[k])
        copy.start()
        return copy

    get_left = local(left_ref, left, 0)
    get_share = local(share_ref, share, 1)
    scalars = [
        local(shift_hbm, shift_ref, 2), local(weight_hbm, weight_ref, 3),
        local(center_hbm, center_ref, 4), local(owner_hbm, owner_ref, 5),
    ]
    get_table = local(rowt_ref, rowt, 6)
    get_mine = local(mine_ref, mine, 7)
    for z in range(planes):
        for c in range(chunks):
            part = (z, pl.ds(c * (height // chunks), height // chunks))
            local(volume_ref.at[part], vol.at[part], 9 + z)
    get_colt = local(colt_ref, colt, 8)

    barrier = pltpu.get_barrier_semaphore()
    for k in range(1, n):
        pl.semaphore_signal(
            barrier, inc=1, device_id={"slab": lax.rem(me + k, n)}, device_id_type=MESH
        )

    def remote(source, into, send, recv, device):
        return pltpu.make_async_remote_copy(
            src_ref=source, dst_ref=into, send_sem=send, recv_sem=recv,
            device_id={"slab": device}, device_id_type=MESH,
        )

    for z in range(planes):
        rows[z, :pad, :] = jnp.zeros((pad, LANES), F32)
        rows[z, pad + width :, :] = jnp.zeros((pad, LANES), F32)
    summed[width:, :] = jnp.zeros((SUBLANES, LANES), F32)
    line[...] = jnp.zeros(line.shape, F32)

    lane = lax.broadcasted_iota(jnp.int32, (LANES, LANES), 1)
    get_left.wait()
    get_share.wait()

    @pl.loop(0, blocks)
    def _(b):
        begin = pl.multiple_of(b * LANES, LANES)
        for t in range(tilts):
            row = left[t : t + 1, pl.ds(begin, LANES)].astype(F32)
            column = jnp.broadcast_to(row, (LANES, LANES)).T.astype(jnp.int32)
            for x in range(blocks):
                hit = jnp.where(column == lane + x * LANES, 1.0, 0.0)
                onehot[t, pl.ds(begin, LANES), x * LANES : (x + 1) * LANES] = hit.astype(BF16)
            row = share[t : t + 1, pl.ds(begin, LANES)]
            shares[t, pl.ds(begin, LANES), :] = jnp.broadcast_to(row, (LANES, LANES)).T

    get_mine.wait()
    for part in range(2):
        perm[:half, :] = mine[0, part, half:, :]
        for k in range(half):
            row = half - k if k else 0
            perm[half + k : half + k + 1, :] = mine[0, part, row : row + 1, :]
        turned = perm[...].T
        for w in range(owners):
            ref_out[w, part * own : (part + 1) * own, :] = turned[w * own : (w + 1) * own]

    get_table.wait()
    for z in range(planes):
        pltpu.make_async_copy(volume_ref.at[z], vol.at[z], sems.at[9 + z]).wait()
        for c in range(chunks):
            out = jnp.dot(
                rowt[...], vol[z, :, c * CHUNK : (c + 1) * CHUNK], preferred_element_type=F32
            )
            out = out[:count] + out[count:]
            for b in range(CHUNK // LANES):
                here = slice(b * LANES, (b + 1) * LANES)
                begin = c * CHUNK + b * LANES
                rows[z, pad + begin : pad + begin + LANES, :] = out[:band, here].T
                extra[z, begin // LANES : begin // LANES + 1, :] = out[band : band + 1, here]

    for copy in scalars:
        copy.wait()
    for t in range(tilts):
        base = jnp.concatenate(
            [left[t : t + 1, b * LANES : (b + 1) * LANES] for b in range(blocks)], axis=0
        )
        right = jnp.concatenate(
            [share[t : t + 1, b * LANES : (b + 1) * LANES] for b in range(blocks)], axis=0
        )
        value = None
        for z in range(planes):
            weight = weight_ref[t, z]
            taps = (
                (1, right * (1.0 - weight)),
                (0, (1.0 - right) * (1.0 - weight) + right * weight),
                (-1, (1.0 - right) * weight),
            )
            for step, factor in taps:
                index = base + (step - shift_ref[t, z])
                spot = index & (LANES - 1)
                block = lax.shift_right_arithmetic(index, int(math.log2(LANES)))
                found = jnp.zeros((blocks, LANES), F32)
                for b in range(blocks):
                    source = jnp.broadcast_to(extra[z, b : b + 1, :], (blocks, LANES))
                    source = jnp.take_along_axis(source, spot, axis=1)
                    found = jnp.where(block == b, source, found)
                value = factor * found if value is None else value + factor * found
        for b in range(blocks):
            line[t : t + 1, b * LANES : (b + 1) * LANES] = value[b : b + 1, :]

    def along(left_hand, right_hand, **kind):
        return lax.dot_general(
            left_hand, right_hand, (((1,), (1,)), ((), ())), preferred_element_type=F32, **kind
        )

    def prepare(t):
        for b in range(blocks):
            total = None
            for z in range(planes):
                weight = weight_ref[t, z]
                start = pad + b * LANES - shift_ref[t, z]
                near = rows[z, pl.ds(start, LANES), :]
                far = rows[z, pl.ds(start - 1, LANES), :]
                term = (1.0 - weight) * near + weight * far
                total = term if total is None else total + term
            here = slice(b * LANES, (b + 1) * LANES)
            summed[here, :] = total
            high, low = halves(total)
            stack[here, 0:LANES] = high
            stack[here, LANES : 2 * LANES] = low
        for b in range(blocks):
            here = slice(b * LANES, (b + 1) * LANES)
            high, low = halves(summed[b * LANES + 1 : (b + 1) * LANES + 1, :])
            stack[here, 2 * LANES : 3 * LANES] = high
            stack[here, 3 * LANES :] = low

    def gather(t):
        for c in range(chunks):
            here = slice(c * CHUNK, (c + 1) * CHUNK)
            picked = jnp.dot(onehot[t, here, :], stack[...], preferred_element_type=F32)
            near = picked[:, :LANES] + picked[:, LANES : 2 * LANES]
            far = picked[:, 2 * LANES : 3 * LANES] + picked[:, 3 * LANES :]
            part = shares[t, here, :]
            high, low = halves((1.0 - part) * near + part * far)
            proj[here, :LANES] = high
            proj[here, LANES:] = low

    def columns(t):
        both = jnp.dot(colt[...], proj[...], preferred_element_type=F32)
        top = 2 * band
        value = both[:top, :LANES] + both[:top, LANES:] + both[top:, :LANES]
        for w in range(owners):
            spec_out[t, w, : 2 * own, :] = value[w * 2 * own : (w + 1) * 2 * own]

    def to_sibling(t):
        return remote(spec_out.at[t], spec_sib.at[t], sib_send, sib_recv, sibling)

    def to_owner(t, w):
        return remote(
            spec_out.at[t, w], spec_in.at[t, chip], spec_send.at[w], spec_recv.at[t], places[w]
        )

    def to_others(make):
        for w in range(owners):
            pl.when(me != places[w])(lambda: make(w).start())

    def ref_to(w):
        return remote(ref_out.at[w], ref_in.at[me], ref_send.at[w], ref_recv, places[w])

    def pass_on(t):
        @pl.when(core == t % 2)
        def _():
            to_sibling(t).wait_recv()
            spec_out[t] = spec_out[t] + spec_sib[t]
            to_others(functools.partial(to_owner, t))

    for t in range(tilts):
        prepare(t)
        if t == 0:
            pl.semaphore_wait(barrier, n - 1)
            to_others(ref_to)
            get_colt.wait()
        gather(t)
        if t:
            pass_on(t - 1)
        else:
            value = line[...]
            high = value.astype(BF16).astype(F32)
            value = jnp.concatenate([high, value - high], axis=0).astype(BF16)
            one = along(value, colt[: 2 * band, :])
            two = along(value, colt[2 * band :, :])
            value = one[:SUBLANES] + one[SUBLANES:] + two[:SUBLANES]
            for w in range(owners):
                begin = w * 2 * own
                offset = begin % LANES
                block = value[:, begin - offset : begin - offset + LANES]
                if offset:
                    block = pltpu.roll(block, LANES - offset, 1)
                for s in range(tilts):
                    spec_out[s, w, 2 * own :, :] = block
        columns(t)

        @pl.when(core != t % 2)
        def _():
            to_sibling(t).start()

    pass_on(tilts - 1)

    def wave(ints):
        angle = (ints & (length - 1)).astype(F32) * (2.0 * math.pi / length)
        return jnp.cos(angle), jnp.sin(angle)

    is_owner = functools.reduce(jnp.logical_or, [me == place for place in places])
    slot = (me - first) // stride

    @pl.when(is_owner)
    def _():
        spot = lax.broadcasted_iota(jnp.int32, (n, band), 1)
        freq = jnp.where(spot < half, spot, jnp.where(spot == half, -half, half - spot))
        step = lax.broadcasted_iota(jnp.int32, (n, band), 0) - n // 2
        cols = lax.broadcasted_iota(jnp.int32, (own, win_cols), 0) + slot * own
        offset = lax.broadcasted_iota(jnp.int32, (own, win_cols), 1) - win_cols // 2
        row_waves, col_waves = [], []
        for t in range(tilts):
            row_waves.append(jnp.concatenate(wave(freq * (center_ref[t, 0] + step)), axis=0))
            cos, sin = wave(cols * (center_ref[t, 1] + offset))
            col_waves.append(jnp.concatenate([cos, -sin], axis=0))
        spot = lax.broadcasted_iota(jnp.int32, (own, band), 1)
        lower, start, middle = spot < half, spot == 0, spot == half
        ref_in[me] = ref_out[slot]
        remote(
            ref_in.at[pl.ds(0, n - 1)], ref_in.at[pl.ds(0, n - 1)], ref_send.at[0], ref_recv, me
        ).wait_recv()
        part_out[tilts * n :, :] = jnp.zeros((SUBLANES, win_cols), F32)
        for t in range(tilts):
            remote_count = n // 2
            if t % 2 == 1:
                spec_in[t, chip] = spec_out[t, slot]
                remote_count -= 1
            arrived = spec_in.at[t, pl.ds(0, remote_count)]
            remote(arrived, arrived, spec_send.at[0], spec_recv.at[t], me).wait_recv()
            total = spec_in[t, 0]
            for e in range(1, n // 2):
                total = total + spec_in[t, e]
            cos, sin = total[:own], total[own : 2 * own]
            last = total[2 * own :].T[:, t : t + 1]
            last_cos, last_sin = last[:own], last[own : 2 * own]
            cos_turn = pltpu.roll(cos, half, 1)
            sin_turn = pltpu.roll(sin, half, 1)
            spec_re = jnp.where(
                lower,
                cos - jnp.where(start, 0.0, sin_turn),
                jnp.where(middle, cos + last_sin, cos_turn + sin),
            )
            spec_im = jnp.where(
                lower,
                -(jnp.where(start, 0.0, cos_turn) + sin),
                jnp.where(middle, last_cos - sin, cos - sin_turn),
            )
            owned = ref_in[owner_ref[t]]
            ref_re, ref_im = owned[:own], owned[own:]
            cross_re = spec_re * ref_re + spec_im * ref_im
            cross_im = spec_im * ref_re - spec_re * ref_im
            for kind, (real, imag) in enumerate(((spec_re, spec_im), (ref_re, ref_im))):
                power = jnp.sum(real * real + imag * imag, axis=0, keepdims=True)
                row = tilts * n + kind * tilts + t
                part_out[row : row + 1, :] = power
            turned = along(
                row_waves[t], jnp.concatenate([cross_re, cross_im], axis=0),
                precision=lax.Precision.HIGHEST,
            )
            moved_re = turned[:n, :own] - turned[n:, own:]
            moved_im = turned[:n, own:] + turned[n:, :own]
            part_out[t * n : (t + 1) * n, :] = jnp.dot(
                jnp.concatenate([moved_re, moved_im], axis=1), col_waves[t],
                precision=lax.Precision.HIGHEST, preferred_element_type=F32,
            )
        for d in range(n):
            @pl.when(me != d)
            def _():
                remote(part_out, part_in.at[slot], part_send.at[d], part_recv.at[slot], d).start()
        part_in[slot] = part_out[...]

    for w in range(owners):
        @pl.when(me != places[w])
        def _():
            remote(part_in.at[w], part_in.at[w], part_send.at[0], part_recv.at[w], me).wait_recv()
    total = part_in[0]
    for w in range(1, owners):
        total = total + part_in[w]
    power = jnp.sum(total[tilts * n :], axis=1, keepdims=True) / (band * band) + 1e-06
    peaks = []
    mine_row = lax.broadcasted_iota(jnp.int32, (n, win_cols), 0) == me
    for t in range(tilts):
        scale = band * jnp.sqrt(power[t : t + 1] * power[tilts + t : tilts + t + 1])
        value = total[t * n : (t + 1) * n]
        row = jnp.sum(jnp.where(mine_row, value, 0.0), axis=0, keepdims=True)
        corr_ref[t] = row / scale
        peaks.append(jnp.max(jnp.max(value, axis=0, keepdims=True), axis=1, keepdims=True) / scale)

    spot = lax.broadcasted_iota(jnp.int32, (1, win_cols), 1)
    best = jnp.broadcast_to(peaks[0], (1, win_cols))
    for t in range(1, tilts):
        best = jnp.where(spot == t, peaks[t], best)
    peak_ref[...] = best[0, :tilts]

    def done(make):
        for w in range(owners):
            pl.when(me != places[w])(lambda: make(w).wait_send())

    done(ref_to)
    for t in range(tilts):
        @pl.when(core == t % 2)
        def _():
            done(functools.partial(to_owner, t))

        @pl.when(core != t % 2)
        def _():
            to_sibling(t).wait_send()

    @pl.when(is_owner)
    def _():
        for d in range(n):
            @pl.when(me != d)
            def _():
                remote(part_out, part_in.at[slot], part_send.at[d], part_recv.at[slot], d).wait_send()


def run(n, volume, shift, weight, left, share, center, owner, mine):
    planes, height, width = volume.shape
    tilts = left.shape[0]
    band = mine.shape[-1]
    win_cols = band
    owners = OWNERS
    rowt = row_table(height, band)
    colt = col_table(width, band, owners)
    blocks = width // LANES
    pad = width // 16 + SUBLANES
    own = band // owners
    message = (2 * own + SUBLANES, band)
    part = (tilts * n + SUBLANES, win_cols)
    smem = pl.BlockSpec(memory_space=pltpu.SMEM)
    vmem = pl.BlockSpec(memory_space=pltpu.VMEM)
    hbm = pl.BlockSpec(memory_space=pl.ANY)
    dma = pltpu.SemaphoreType.DMA
    return pl.pallas_call(
        functools.partial(fused_kernel, n, owners),
        out_shape=(
            pltpu.VMEM((tilts, 1, win_cols), F32),
            pltpu.VMEM((tilts,), F32),
        ),
        in_specs=[hbm] * 10,
        out_specs=(vmem, vmem),
        scratch_shapes=[
            pltpu.SMEM(center.shape, jnp.int32),
            pltpu.SMEM(owner.shape, jnp.int32),
            pltpu.SMEM(shift.shape, jnp.int32),
            pltpu.SMEM(weight.shape, F32),
            pltpu.VMEM(left.shape, jnp.int32),
            pltpu.VMEM(share.shape, F32),
            pltpu.VMEM(mine.shape, F32),
            pltpu.VMEM((planes, height, width), BF16),
            pltpu.VMEM(rowt.shape, BF16),
            pltpu.VMEM(colt.shape, BF16),
            pltpu.VMEM((tilts, width, width), BF16),
            pltpu.VMEM((tilts, width, LANES), F32),
            pltpu.VMEM((planes, width + 2 * pad, LANES), F32),
            pltpu.VMEM((planes, blocks, LANES), F32),
            pltpu.VMEM((SUBLANES, width), F32),
            pltpu.VMEM((width + SUBLANES, LANES), F32),
            pltpu.VMEM((width, 4 * LANES), BF16),
            pltpu.VMEM((width, 2 * LANES), BF16),
            pltpu.VMEM((band, band), F32),
            pltpu.VMEM((owners, 2 * own, band), F32),
            pltpu.VMEM((n, 2 * own, band), F32),
            pltpu.VMEM((tilts, owners) + message, F32),
            pltpu.VMEM((tilts, owners) + message, F32),
            pltpu.VMEM((tilts, n // 2) + message, F32),
            pltpu.VMEM(part, F32),
            pltpu.VMEM((owners,) + part, F32),
            dma((9 + planes,)),
            dma((owners,)), dma, dma, dma,
            dma((owners,)), dma((tilts,)), dma((n,)), dma((owners,)),
        ],
        compiler_params=pltpu.CompilerParams(
            collective_id=0, has_side_effects=True, vmem_limit_bytes=56 * 1024 * 1024
        ),
        name="fused",
    )(
        center, owner, shift, weight, left, share, mine,
        volume, jnp.asarray(rowt), jnp.asarray(colt),
    )


def solution(mesh):
    n = mesh.shape["slab"]

    def per_device(volume, shift, weight, left, share, center, owner, bands):
        return run(n, volume, shift, weight, left, share, center, owner, bands)

    placed = (
        P(("grp", "slab"), None, None),
        P("grp", "slab"),
        P("grp", "slab"),
        P("grp", None),
        P("grp", None),
        P("grp", None),
        P("grp"),
        P(("grp", "slab"), None, None, None),
    )
    return jax.shard_map(
        per_device,
        mesh=mesh,
        in_specs=placed,
        out_specs=(P("grp", "slab", None), P("grp")),
        check_vma=False,
    )
```

time: 32.1 us -> 23.5 us (0.73)
  Pallas kernels: 31.4 us -> 21.5 us
  local copies, waits for them, and re-layouts: 0 us -> 1.08 us
    pallas_call x2 -> x1, Pallas kernels: 31.4 us -> 21.5 us  [run(): pl.pallas_call(functools.partial(fused_kernel, n, owners), out_shape=(plt...]
    unnamed x0 -> x2, local copies, waits for them, and re-layouts: none -> 1.08 us
where the time goes in v1:
time: 23.5 us; the launch traced here: 23.3 us
  Pallas kernels  21.5 us (91%)
  local copies, waits for them, and re-layouts  1.08 us (5%)
  between operations  0.64 us (3%)
    pallas_call x1, Pallas kernels, run(): pl.pallas_call(functools.partial(fused_kernel, n, owners), out_shape=(plt...  21.5 us
    unnamed x2, local copies, waits for them, and re-layouts  1.08 us

profile of v1, /device:TPU:0, one launch (start us, length us, event | category | flops | bytes accessed | tf_op | source)
XLA Modules:
  0.0 23.3 jit_solution(1021928874962525137)
XLA Ops:
  0.6 21.5 %fused.1 = (f32[2,1,128]{2,1,0:T(1,128)S(1)}, f32[2]{0:T(128)S(1)}) custom-call(s32[2,2]{1,0:T(2,128)} %center_hbm.1, s32[16]{0:T(128)} %owner_hbm.1, s32[2,2]{1,0:T(2,128)} %shift_hbm.1, f32[2,2]{1,0:T(2,128)} %weight_hbm.1, s32[2,1024]{1,0:T(2,128)} %left_ref.1, f32[2,1024]{1,0:T(2,128)} %share_ref.1, f32[1,2,128,128]{3,2,1,0:T(8,128)} %mine_ref.1, ...), custom_call_target="tpu_custom_call" | custom-call | tf_op jit(solution)/shard_map/fused/pallas_call | solution.py:421
  22.2 0.6 %copy.14 = f32[2,1,128]{2,1,0:T(1,128)} copy(f32[2,1,128]{2,1,0:T(1,128)S(1)} %get-tuple-element.2) | data formatting | bytes 2048
  22.8 0.5 %copy.15 = f32[2]{0:T(128)} copy(f32[2]{0:T(128)S(1)} %get-tuple-element.3) | data formatting | bytes 16

commit v2 on v1

v2 whole, which is shorter than its diff:
```python
import functools
import math

import jax
import jax.numpy as jnp
import numpy as np
from jax import lax
from jax.experimental import pallas as pl
from jax.experimental.pallas import tpu as pltpu
from jax.sharding import PartitionSpec as P

MESH = pl.DeviceIdType.MESH
LANES = 128
SUBLANES = 8
CHUNK = 256
OWNERS = 4
PIECES = 4
BF16 = jnp.bfloat16
F32 = jnp.float32


def phases(left, right, length):
    angle = (np.outer(left, right) % length) * (2.0 * math.pi / length)
    return np.cos(angle), np.sin(angle)


def split(values):
    high = values.astype(np.float32).astype(BF16)
    low = (values - high.astype(np.float64)).astype(np.float32).astype(BF16)
    return high, low


def halves(value):
    high = value.astype(BF16)
    return high, (value - high.astype(F32)).astype(BF16)


def row_table(length, band):
    half = band // 2
    cos, sin = phases(np.arange(half + 1), np.arange(length), length)
    last = np.zeros((SUBLANES, length))
    last[0] = sin[half]
    return np.concatenate(split(np.concatenate([cos[:half], cos[half:], sin[1:half], last])))


def col_table(length, band, owners):
    cos, sin = phases(np.arange(band), np.arange(length), length)
    own = band // owners
    rows = []
    for w in range(owners):
        rows += [cos[w * own : (w + 1) * own], sin[w * own : (w + 1) * own]]
    return np.concatenate(split(np.concatenate(rows)))


def fused_kernel(
    n, owners, center_hbm, owner_hbm, shift_hbm, weight_hbm,
    left_ref, share_ref, mine_ref, volume_ref, rowt_ref, colt_ref, out_ref,
    center_ref, owner_ref, shift_ref, weight_ref, left, share, mine, vol, rowt, colt,
    onehot, shares, rows, extra, line, summed, give, take, stack, proj,
    perm, line_keep, line_give, line_take, ref_out, ref_in, spec_out, spec_in, part_out, part_in,
    sems, ref_send, ref_recv, sib_send, sib_recv, line_send, line_recv,
    spec_send, spec_recv, part_send, part_recv,
):
    me = lax.axis_index("slab")
    core = lax.rem(me, 2)
    sibling = me + 1 - 2 * core
    chip = me // 2
    planes, height, width = volume_ref.shape
    tilts = left_ref.shape[0]
    pairs = tilts // 2
    band = mine_ref.shape[-1]
    half = band // 2
    own = band // owners
    blocks = width // LANES
    chunks = width // CHUNK
    pieces = give.shape[1]
    count = rowt_ref.shape[0] // 2
    pad = (rows.shape[1] - width) // 2
    length = width
    win_cols = out_ref.shape[-1]
    first, stride = n // owners + 1, max(2, n // (2 * owners))
    places = [first + w * stride for w in range(owners)]

    barrier = pltpu.get_barrier_semaphore()
    for k in range(1, n):
        pl.semaphore_signal(
            barrier, inc=1, device_id={"slab": lax.rem(me + k, n)}, device_id_type=MESH
        )

    def local(source, into, k):
        copy = pltpu.make_async_copy(source, into, sems.at[k])
        copy.start()
        return copy

    get_left = local(left_ref, left, 0)
    get_share = local(share_ref, share, 1)
    scalars = [
        local(shift_hbm, shift_ref, 2), local(weight_hbm, weight_ref, 3),
        local(center_hbm, center_ref, 4), local(owner_hbm, owner_ref, 5),
    ]
    get_table = local(rowt_ref, rowt, 6)
    get_mine = local(mine_ref, mine, 7)
    for z in range(planes):
        for c in range(chunks):
            part = (z, pl.ds(c * (height // chunks), height // chunks))
            local(volume_ref.at[part], vol.at[part], 9 + z)
    get_colt = local(colt_ref, colt, 8)

    def remote(source, into, send, recv, device):
        return pltpu.make_async_remote_copy(
            src_ref=source, dst_ref=into, send_sem=send, recv_sem=recv,
            device_id={"slab": device}, device_id_type=MESH,
        )

    for z in range(planes):
        rows[z, :pad, :] = jnp.zeros((pad, LANES), F32)
        rows[z, pad + width :, :] = jnp.zeros((pad, LANES), F32)
    summed[width:, :] = jnp.zeros((SUBLANES, LANES), F32)

    def row_of(ref, t, here):
        value = ref[0:1, here]
        for k in range(1, tilts):
            value = jnp.where(t == k, ref[k : k + 1, here], value)
        return value

    lane = lax.broadcasted_iota(jnp.int32, (LANES, LANES), 1)
    get_left.wait()
    get_share.wait()

    @pl.loop(0, blocks)
    def _(b):
        begin = pl.multiple_of(b * LANES, LANES)
        for i in range(pairs):
            t = 2 * i + core
            row = row_of(left, t, pl.ds(begin, LANES)).astype(F32)
            column = jnp.broadcast_to(row, (LANES, LANES)).T.astype(jnp.int32)
            for x in range(blocks):
                hit = jnp.where(column == lane + x * LANES, 1.0, 0.0)
                onehot[i, pl.ds(begin, LANES), x * LANES : (x + 1) * LANES] = hit.astype(BF16)
            row = row_of(share, t, pl.ds(begin, LANES))
            shares[i, pl.ds(begin, LANES), :] = jnp.broadcast_to(row, (LANES, LANES)).T

    get_mine.wait()
    for part in range(2):
        perm[:half, :] = mine[0, part, half:, :]
        for k in range(half):
            row = half - k if k else 0
            perm[half + k : half + k + 1, :] = mine[0, part, row : row + 1, :]
        turned = perm[...].T
        for w in range(owners):
            ref_out[w, part * own : (part + 1) * own, :] = turned[w * own : (w + 1) * own]

    def last_row(t):
        base = jnp.concatenate(
            [row_of(left, t, slice(b * LANES, (b + 1) * LANES)) for b in range(blocks)], axis=0
        )
        right = jnp.concatenate(
            [row_of(share, t, slice(b * LANES, (b + 1) * LANES)) for b in range(blocks)], axis=0
        )
        value = None
        for z in range(planes):
            weight = weight_ref[t, z]
            taps = (
                (1, right * (1.0 - weight)),
                (0, (1.0 - right) * (1.0 - weight) + right * weight),
                (-1, (1.0 - right) * weight),
            )
            for step, factor in taps:
                index = base + (step - shift_ref[t, z])
                spot = index & (LANES - 1)
                block = lax.shift_right_arithmetic(index, int(math.log2(LANES)))
                found = jnp.zeros((blocks, LANES), F32)
                for b in range(blocks):
                    source = jnp.broadcast_to(extra[z, b : b + 1, :], (blocks, LANES))
                    source = jnp.take_along_axis(source, spot, axis=1)
                    found = jnp.where(block == b, source, found)
                value = factor * found if value is None else value + factor * found
        return value

    def shifted(t, begin, size):
        total = None
        for z in range(planes):
            weight = weight_ref[t, z]
            start = pad + begin - shift_ref[t, z]
            near = rows[z, pl.ds(start, size), :]
            far = rows[z, pl.ds(start - 1, size), :]
            term = (1.0 - weight) * near + weight * far
            total = term if total is None else total + term
        return total

    def along(left_hand, right_hand):
        return lax.dot_general(
            left_hand, right_hand, (((1,), (1,)), ((), ())), preferred_element_type=F32
        )

    def to_sibling(i, k):
        return remote(
            give.at[i, k], take.at[i, k], sib_send.at[i], sib_recv.at[i, k], sibling
        )

    def to_owner(i, w):
        used = pl.ds(0, 2 * own + 1)
        t = 2 * i + core
        return remote(
            spec_out.at[i, w, used], spec_in.at[t, chip, used],
            spec_send.at[i], spec_recv.at[t], places[w],
        )

    def to_others(make):
        for w in range(owners):
            pl.when(me != places[w])(lambda: make(w).start())

    refs = pl.ds(0, 2 * own)

    def ref_to(w):
        return remote(ref_out.at[w], ref_in.at[me, refs], ref_send, ref_recv, places[w])

    span = width // pieces

    def row_chunk(z, c):
        out = jnp.dot(
            rowt[...], vol[z, :, c * CHUNK : (c + 1) * CHUNK], preferred_element_type=F32
        )
        out = out[:count] + out[count:]
        for b in range(CHUNK // LANES):
            here = slice(b * LANES, (b + 1) * LANES)
            begin = c * CHUNK + b * LANES
            rows[z, pad + begin : pad + begin + LANES, :] = out[:band, here].T
            extra[z, begin // LANES : begin // LANES + 1, :] = out[band : band + 1, here]

    def give_piece(k):
        for i in range(pairs):
            for b in range(span // LANES):
                here = slice(b * LANES, (b + 1) * LANES)
                give[i, k, here, :] = shifted(2 * i + 1 - core, k * span + b * LANES, LANES)
            to_sibling(i, k).start()

    def own_part(i):
        t = 2 * i + core
        for b in range(blocks):
            summed[b * LANES : (b + 1) * LANES, :] = shifted(t, b * LANES, LANES)

    def line_copy(i):
        return remote(line_give.at[i], line_take.at[i], line_send.at[i], line_recv.at[i], sibling)

    def last_line(i):
        line[...] = jnp.zeros(line.shape, F32)
        for k, t in enumerate((2 * i + core, 2 * i + 1 - core)):
            value = last_row(t)
            for b in range(blocks):
                line[k : k + 1, b * LANES : (b + 1) * LANES] = value[b : b + 1, :]
        value = line[...]
        high = value.astype(BF16).astype(F32)
        value = jnp.concatenate([high, value - high], axis=0).astype(BF16)
        one = along(value, colt[: 2 * band, :])
        two = along(value, colt[2 * band :, :])
        value = one[:SUBLANES] + one[SUBLANES:] + two[:SUBLANES]
        line_give[i] = jnp.zeros((SUBLANES, LANES), F32)
        for k in range(2 * band // LANES):
            here = slice(k * LANES, (k + 1) * LANES)
            line_keep[i, k : k + 1, :] = value[0:1, here]
            line_give[i, k : k + 1, :] = value[1:2, here]
        line_copy(i).start()

    def merge(i):
        def near(b):
            here = slice(b * LANES, (b + 1) * LANES)
            begin = (b * LANES) % span
            total = summed[here, :] + take[i, b * LANES // span, begin : begin + LANES, :]
            summed[here, :] = total
            high, low = halves(total)
            stack[here, 0:LANES] = high
            stack[here, LANES : 2 * LANES] = low

        def far(b):
            here = slice(b * LANES, (b + 1) * LANES)
            high, low = halves(summed[b * LANES + 1 : (b + 1) * LANES + 1, :])
            stack[here, 2 * LANES : 3 * LANES] = high
            stack[here, 3 * LANES :] = low

        each = span // LANES
        for k in range(pieces):
            to_sibling(i, k).wait_recv()
            for b in range(k * each, (k + 1) * each):
                near(b)
                if b:
                    far(b - 1)
        far(blocks - 1)

    def put_line(i):
        line_copy(i).wait_recv()
        for w in range(owners):
            begin = w * 2 * own
            offset = begin % LANES
            k = begin // LANES
            block = line_keep[i, k : k + 1, :] + line_take[i, k : k + 1, :]
            if offset:
                block = pltpu.roll(jnp.broadcast_to(block, (SUBLANES, LANES)), LANES - offset, 1)
            spec_out[i, w, 2 * own : 2 * own + 1, :] = block[0:1]

    def gather(i):
        for c in range(chunks):
            here = slice(c * CHUNK, (c + 1) * CHUNK)
            picked = jnp.dot(onehot[i, here, :], stack[...], preferred_element_type=F32)
            near = picked[:, :LANES] + picked[:, LANES : 2 * LANES]
            far = picked[:, 2 * LANES : 3 * LANES] + picked[:, 3 * LANES :]
            part = shares[i, here, :]
            high, low = halves((1.0 - part) * near + part * far)
            proj[here, :LANES] = high
            proj[here, LANES:] = low

    def columns(i):
        both = jnp.dot(colt[...], proj[...], preferred_element_type=F32)
        top = 2 * band
        value = both[:top, :LANES] + both[:top, LANES:] + both[top:, :LANES]
        for w in range(owners):
            spec_out[i, w, : 2 * own, :] = value[w * 2 * own : (w + 1) * 2 * own]

    for copy in scalars:
        copy.wait()
    get_table.wait()
    sent = 0
    for z in range(planes):
        pltpu.make_async_copy(volume_ref.at[z], vol.at[z], sems.at[9 + z]).wait()
        for c in range(chunks):
            row_chunk(z, c)
            if z == planes - 1 and c >= chunks // 2:
                if not sent:
                    pl.semaphore_wait(barrier, n - 1)
                ready = pieces if c == chunks - 1 else c * CHUNK // span
                for k in range(sent, ready):
                    give_piece(k)
                sent = ready
    to_others(ref_to)
    get_colt.wait()
    for i in range(pairs):
        last_line(i)
    for i in range(pairs):
        own_part(i)
        merge(i)
        gather(i)
        columns(i)
        put_line(i)
        to_others(functools.partial(to_owner, i))

    def wave(ints):
        angle = (ints & (length - 1)).astype(F32) * (2.0 * math.pi / length)
        return jnp.cos(angle), jnp.sin(angle)

    def thirds(value, axis, order):
        high = value.astype(BF16)
        parts = (high, (value - high.astype(F32)).astype(BF16))
        return jnp.concatenate([parts[k] for k in order], axis=axis)

    is_owner = functools.reduce(jnp.logical_or, [me == place for place in places])
    slot = (me - first) // stride

    @pl.when(is_owner)
    def _():
        spot = lax.broadcasted_iota(jnp.int32, (n, band), 1)
        freq = jnp.where(spot < half, spot, jnp.where(spot == half, -half, half - spot))
        step = lax.broadcasted_iota(jnp.int32, (n, band), 0) - n // 2
        cols = lax.broadcasted_iota(jnp.int32, (own, win_cols), 0) + slot * own
        offset = lax.broadcasted_iota(jnp.int32, (own, win_cols), 1) - win_cols // 2
        row_waves, col_waves = [], []
        for t in range(tilts):
            waves = jnp.concatenate(wave(freq * (center_ref[t, 0] + step)), axis=0)
            row_waves.append(thirds(waves, 1, (0, 0, 1)))
            cos, sin = wave(cols * (center_ref[t, 1] + offset))
            col_waves.append(thirds(jnp.concatenate([cos, -sin], axis=0), 0, (0, 1, 0)))
        spot = lax.broadcasted_iota(jnp.int32, (own, band), 1)
        lower, start, middle = spot < half, spot == 0, spot == half
        ref_in[me, refs] = ref_out[slot]
        arrived = ref_in.at[pl.ds(0, n - 1), refs]
        remote(arrived, arrived, ref_send, ref_recv, me).wait_recv()
        part_out[tilts * n :, :] = jnp.zeros((SUBLANES, win_cols), F32)

        def put_power(real, imag, row):
            power = jnp.sum(real * real + imag * imag, axis=0, keepdims=True)
            part_out[tilts * n + row : tilts * n + row + 1, :] = power

        owned = [ref_in[owner_ref[t], refs] for t in range(tilts)]
        for t in range(tilts):
            put_power(owned[t][:own], owned[t][own:], tilts + t)
        used = pl.ds(0, 2 * own + 1)
        for t in [*range(1, tilts, 2), *range(0, tilts, 2)]:
            remote_count = n // 2
            if t % 2 == 1:
                spec_in[t, chip, used] = spec_out[t // 2, slot, used]
                remote_count -= 1
            arrived = spec_in.at[t, pl.ds(0, remote_count), used]
            remote(arrived, arrived, spec_send.at[0], spec_recv.at[t], me).wait_recv()
        for t in range(tilts):
            total = spec_in[t, 0, : 2 * own]
            last = spec_in[t, 0, 2 * own : 2 * own + 1]
            for e in range(1, n // 2):
                total = total + spec_in[t, e, : 2 * own]
                last = last + spec_in[t, e, 2 * own : 2 * own + 1]
            cos, sin = total[:own], total[own:]
            last = jnp.broadcast_to(last, (SUBLANES, band)).T[:, 0:1]
            last_cos, last_sin = last[:own], last[own : 2 * own]
            cos_turn = pltpu.roll(cos, half, 1)
            sin_turn = pltpu.roll(sin, half, 1)
            spec_re = jnp.where(
                lower,
                cos - jnp.where(start, 0.0, sin_turn),
                jnp.where(middle, cos + last_sin, cos_turn + sin),
            )
            spec_im = jnp.where(
                lower,
                -(jnp.where(start, 0.0, cos_turn) + sin),
                jnp.where(middle, last_cos - sin, cos - sin_turn),
            )
            ref_re, ref_im = owned[t][:own], owned[t][own:]
            cross_re = spec_re * ref_re + spec_im * ref_im
            cross_im = spec_im * ref_re - spec_re * ref_im
            put_power(spec_re, spec_im, t)
            turned = along(
                row_waves[t],
                thirds(jnp.concatenate([cross_re, cross_im], axis=0), 1, (0, 1, 0)),
            )
            moved_re = turned[:n, :own] - turned[n:, own:]
            moved_im = turned[:n, own:] + turned[n:, :own]
            part_out[t * n : (t + 1) * n, :] = jnp.dot(
                thirds(jnp.concatenate([moved_re, moved_im], axis=1), 1, (0, 0, 1)),
                col_waves[t], preferred_element_type=F32,
            )
        for d in range(n):
            @pl.when(me != d)
            def _():
                remote(part_out, part_in.at[slot], part_send, part_recv, d).start()
        part_in[slot] = part_out[...]

    def settle(ref, send, recv, sending):
        for fewer in range(2):
            @pl.when(is_owner == (fewer == 1))
            def _():
                part = ref.at[pl.ds(0, owners - fewer)]
                copy = remote(part, part, send, recv, me)
                if sending:
                    copy.wait_send()
                else:
                    copy.wait_recv()

    settle(part_in, part_send, part_recv, False)
    total = part_in[0]
    for w in range(1, owners):
        total = total + part_in[w]
    power = jnp.sum(total[tilts * n :], axis=1, keepdims=True) / (band * band) + 1e-06
    peaks = []
    mine_row = lax.broadcasted_iota(jnp.int32, (n, win_cols), 0) == me
    for t in range(tilts):
        scale = band * jnp.sqrt(power[t : t + 1] * power[tilts + t : tilts + t + 1])
        value = total[t * n : (t + 1) * n]
        row = jnp.sum(jnp.where(mine_row, value, 0.0), axis=0, keepdims=True)
        out_ref[t] = row / scale
        peaks.append(jnp.max(jnp.max(value, axis=0, keepdims=True), axis=1, keepdims=True) / scale)
    spot = lax.broadcasted_iota(jnp.int32, (1, win_cols), 1)
    best = jnp.broadcast_to(peaks[0], (1, win_cols))
    for t in range(1, tilts):
        best = jnp.where(spot == t, peaks[t], best)
    out_ref[tilts] = best

    settle(ref_out, ref_send, ref_recv, True)
    for i in range(pairs):
        remote(give.at[i], take.at[i], sib_send.at[i], sib_recv.at[i, 0], sibling).wait_send()
        line_copy(i).wait_send()
        settle(spec_out.at[i, :, pl.ds(0, 2 * own + 1)], spec_send.at[i], spec_recv.at[0], True)

    @pl.when(is_owner)
    def _():
        every = ref_in.at[pl.ds(0, n - 1), pl.ds(0, part_out.shape[0])]
        remote(every, every, part_send, part_recv, me).wait_send()


def finish_kernel(both_ref, corr_ref, peak_ref):
    tilts = corr_ref.shape[0]
    corr_ref[...] = both_ref[:tilts]
    peak_ref[...] = both_ref[tilts, 0, :tilts]


def run(n, volume, shift, weight, left, share, center, owner, mine):
    planes, height, width = volume.shape
    tilts = left.shape[0]
    pairs = tilts // 2
    band = mine.shape[-1]
    win_cols = band
    owners = OWNERS
    rowt = row_table(height, band)
    colt = col_table(width, band, owners)
    blocks = width // LANES
    pad = width // 16 + SUBLANES
    own = band // owners
    message = (2 * own + SUBLANES, band)
    part = (tilts * n + SUBLANES, win_cols)
    smem = pl.BlockSpec(memory_space=pltpu.SMEM)
    vmem = pl.BlockSpec(memory_space=pltpu.VMEM)
    hbm = pl.BlockSpec(memory_space=pl.ANY)
    dma = pltpu.SemaphoreType.DMA
    both = pl.pallas_call(
        functools.partial(fused_kernel, n, owners),
        out_shape=pltpu.VMEM((tilts + 1, 1, win_cols), F32),
        in_specs=[hbm] * 10,
        out_specs=vmem,
        scratch_shapes=[
            pltpu.SMEM(center.shape, jnp.int32),
            pltpu.SMEM(owner.shape, jnp.int32),
            pltpu.SMEM(shift.shape, jnp.int32),
            pltpu.SMEM(weight.shape, F32),
            pltpu.VMEM(left.shape, jnp.int32),
            pltpu.VMEM(share.shape, F32),
            pltpu.VMEM(mine.shape, F32),
            pltpu.VMEM((planes, height, width), BF16),
            pltpu.VMEM(rowt.shape, BF16),
            pltpu.VMEM(colt.shape, BF16),
            pltpu.VMEM((pairs, width, width), BF16),
            pltpu.VMEM((pairs, width, LANES), F32),
            pltpu.VMEM((planes, width + 2 * pad, LANES), F32),
            pltpu.VMEM((planes, blocks, LANES), F32),
            pltpu.VMEM((SUBLANES, width), F32),
            pltpu.VMEM((width + SUBLANES, LANES), F32),
            pltpu.VMEM((pairs, PIECES, width // PIECES, LANES), F32),
            pltpu.VMEM((pairs, PIECES, width // PIECES, LANES), F32),
            pltpu.VMEM((width, 4 * LANES), BF16),
            pltpu.VMEM((width, 2 * LANES), BF16),
            pltpu.VMEM((band, band), F32),
            pltpu.VMEM((pairs, SUBLANES, LANES), F32),
            pltpu.VMEM((pairs, SUBLANES, LANES), F32),
            pltpu.VMEM((pairs, SUBLANES, LANES), F32),
            pltpu.VMEM((owners, 2 * own, band), F32),
            pltpu.VMEM((n, max(2 * own, part[0]), band), F32),
            pltpu.VMEM((pairs, owners) + message, F32),
            pltpu.VMEM((tilts, n // 2) + message, F32),
            pltpu.VMEM(part, F32),
            pltpu.VMEM((owners,) + part, F32),
            dma((9 + planes,)),
            dma, dma, dma((pairs,)), dma((pairs, PIECES)), dma((pairs,)), dma((pairs,)),
            dma((pairs,)), dma((tilts,)), dma, dma,
        ],
        compiler_params=pltpu.CompilerParams(
            collective_id=0, has_side_effects=True, vmem_limit_bytes=56 * 1024 * 1024
        ),
        name="fused",
    )(
        center, owner, shift, weight, left, share, mine,
        volume, jnp.asarray(rowt), jnp.asarray(colt),
    )
    both = pltpu.with_memory_space_constraint(both, pltpu.VMEM)
    return pl.pallas_call(
        finish_kernel,
        out_shape=(
            jax.ShapeDtypeStruct((tilts, 1, win_cols), F32),
            jax.ShapeDtypeStruct((tilts,), F32),
        ),
        in_specs=[vmem],
        out_specs=(vmem, vmem),
        name="finish",
    )(both)


def solution(mesh):
    n = mesh.shape["slab"]

    def per_device(volume, shift, weight, left, share, center, owner, bands):
        return run(n, volume, shift, weight, left, share, center, owner, bands)

    placed = (
        P(("grp", "slab"), None, None),
        P("grp", "slab"),
        P("grp", "slab"),
        P("grp", None),
        P("grp", None),
        P("grp", None),
        P("grp"),
        P(("grp", "slab"), None, None, None),
    )
    return jax.shard_map(
        per_device,
        mesh=mesh,
        in_specs=placed,
        out_specs=(P("grp", "slab", None), P("grp")),
        check_vma=False,
    )
```

time: 23.5 us -> 21.4 us (0.911)
  local copies, waits for them, and re-layouts: 1.08 us -> 0 us
  Pallas kernels: 21.5 us -> 20.6 us
    unnamed x2 -> x0, local copies, waits for them, and re-layouts: 1.08 us -> none
    pallas_call x1 -> x2, Pallas kernels: 21.5 us -> 20.6 us  [the longest x1 20 us: run(): pl.pallas_call(functools.partial(fused_kernel, n, owners), out_shape=pltp...]
where the time goes in v2:
time: 21.4 us; the launch traced here: 21.2 us
  Pallas kernels  20.6 us (96%)
  between operations  0.64 us (3%)
    pallas_call x1, Pallas kernels, run(): pl.pallas_call(functools.partial(fused_kernel, n, owners), out_shape=pltp...  20 us
    pallas_call x1, Pallas kernels, run(): pl.pallas_call(finish_kernel, out_shape=(jax.ShapeDtypeStruct((tilts, 1,...  0.57 us

profile of v2, /device:TPU:0, one launch (start us, length us, event | category | flops | bytes accessed | tf_op | source)
XLA Modules:
  0.0 21.2 jit_solution(12407572735186911624)
XLA Ops:
  0.6 20.0 %fused.1.both_ref = f32[3,1,128]{2,1,0:T(1,128)S(1)} custom-call(s32[2,2]{1,0:T(2,128)} %center_hbm.1, s32[16]{0:T(128)} %owner_hbm.1, s32[2,2]{1,0:T(2,128)} %shift_hbm.1, f32[2,2]{1,0:T(2,128)} %weight_hbm.1, s32[2,1024]{1,0:T(2,128)} %left_ref.1, f32[2,1024]{1,0:T(2,128)} %share_ref.1, f32[1,2,128,128]{3,2,1,0:T(8,128)} %mine_ref.1, ...), custom_call_target="tpu_custom_call" | custom-call | tf_op jit(solution)/shard_map/fused/pallas_call | solution.py:500
  20.7 0.6 %finish.1 = (f32[2,1,128]{2,1,0:T(1,128)}, f32[2]{0:T(128)}) custom-call(f32[3,1,128]{2,1,0:T(1,128)S(1)} %fused.1.both_ref), custom_call_target="tpu_custom_call" | custom-call | tf_op jit(solution)/shard_map/finish/pallas_call | solution.py:549

commit v3 on v2

--- a/solution.py
+++ b/solution.py
@@ -14,7 +14,8 @@
 SUBLANES = 8
 CHUNK = 256
 OWNERS = 4
-PIECES = 4
+PIECES = 8
+HALVES = 2
 BF16 = jnp.bfloat16
 F32 = jnp.float32
 
@@ -81,16 +82,37 @@
     first, stride = n // owners + 1, max(2, n // (2 * owners))
     places = [first + w * stride for w in range(owners)]
 
+    is_owner = functools.reduce(jnp.logical_or, [me == place for place in places])
+    beside = functools.reduce(jnp.logical_or, [sibling == place for place in places])
     barrier = pltpu.get_barrier_semaphore()
-    for k in range(1, n):
+
+    def greet(device):
         pl.semaphore_signal(
-            barrier, inc=1, device_id={"slab": lax.rem(me + k, n)}, device_id_type=MESH
-        )
+            barrier, inc=1, device_id={"slab": device}, device_id_type=MESH
+        )
+
+    @pl.when(is_owner)
+    def _():
+        for k in range(1, n):
+            greet(lax.rem(me + k, n))
+
+    @pl.when(jnp.logical_not(is_owner))
+    def _():
+        for place in places:
+            greet(place)
+        pl.when(jnp.logical_not(beside))(lambda: greet(sibling))
+
+    def wait_entry():
+        others = owners + jnp.where(beside, 0, 1)
+        pl.semaphore_wait(barrier, jnp.where(is_owner, n - 1, others))
 
     def local(source, into, k):
         copy = pltpu.make_async_copy(source, into, sems.at[k])
         copy.start()
         return copy
+
+    def columns_of(h):
+        return pl.ds(h * (width // HALVES), width // HALVES)
 
     get_left = local(left_ref, left, 0)
     get_share = local(share_ref, share, 1)
@@ -99,11 +121,12 @@
         local(center_hbm, center_ref, 4), local(owner_hbm, owner_ref, 5),
     ]
     get_table = local(rowt_ref, rowt, 6)
+    for h in range(HALVES):
+        for z in range(planes):
+            for c in range(chunks):
+                part = (z, pl.ds(c * (height // chunks), height // chunks), columns_of(h))
+                local(volume_ref.at[part], vol.at[part], 9 + h)
     get_mine = local(mine_ref, mine, 7)
-    for z in range(planes):
-        for c in range(chunks):
-            part = (z, pl.ds(c * (height // chunks), height // chunks))
-            local(volume_ref.at[part], vol.at[part], 9 + z)
     get_colt = local(colt_ref, colt, 8)
 
     def remote(source, into, send, recv, device):
@@ -127,8 +150,7 @@
     get_left.wait()
     get_share.wait()
 
-    @pl.loop(0, blocks)
-    def _(b):
+    def hits(b):
         begin = pl.multiple_of(b * LANES, LANES)
         for i in range(pairs):
             t = 2 * i + core
@@ -140,15 +162,18 @@
             row = row_of(share, t, pl.ds(begin, LANES))
             shares[i, pl.ds(begin, LANES), :] = jnp.broadcast_to(row, (LANES, LANES)).T
 
-    get_mine.wait()
-    for part in range(2):
-        perm[:half, :] = mine[0, part, half:, :]
-        for k in range(half):
-            row = half - k if k else 0
-            perm[half + k : half + k + 1, :] = mine[0, part, row : row + 1, :]
-        turned = perm[...].T
-        for w in range(owners):
-            ref_out[w, part * own : (part + 1) * own, :] = turned[w * own : (w + 1) * own]
+    pl.loop(0, blocks)(hits)
+
+    def prepare_ref():
+        get_mine.wait()
+        for part in range(2):
+            perm[:half, :] = mine[0, part, half:, :]
+            for k in range(half):
+                row = half - k if k else 0
+                perm[half + k : half + k + 1, :] = mine[0, part, row : row + 1, :]
+            turned = perm[...].T
+            for w in range(owners):
+                ref_out[w, part * own : (part + 1) * own, :] = turned[w * own : (w + 1) * own]
 
     def last_row(t):
         base = jnp.concatenate(
@@ -316,21 +341,24 @@
         for w in range(owners):
             spec_out[i, w, : 2 * own, :] = value[w * 2 * own : (w + 1) * 2 * own]
 
+    get_table.wait()
     for copy in scalars:
         copy.wait()
-    get_table.wait()
     sent = 0
-    for z in range(planes):
-        pltpu.make_async_copy(volume_ref.at[z], vol.at[z], sems.at[9 + z]).wait()
-        for c in range(chunks):
-            row_chunk(z, c)
-            if z == planes - 1 and c >= chunks // 2:
-                if not sent:
-                    pl.semaphore_wait(barrier, n - 1)
-                ready = pieces if c == chunks - 1 else c * CHUNK // span
-                for k in range(sent, ready):
-                    give_piece(k)
-                sent = ready
+    for h in range(HALVES):
+        part = (slice(None), slice(None), columns_of(h))
+        pltpu.make_async_copy(volume_ref.at[part], vol.at[part], sems.at[9 + h]).wait()
+        for z in range(planes):
+            for c in range(chunks // HALVES):
+                row_chunk(z, h * (chunks // HALVES) + c)
+        if h == 0:
+            wait_entry()
+        known = (h + 1) * (width // HALVES)
+        ready = pieces if known == width else (known - pad) // span
+        for k in range(sent, ready):
+            give_piece(k)
+        sent = ready
+    prepare_ref()
     to_others(ref_to)
     get_colt.wait()
     for i in range(pairs):
@@ -352,7 +380,6 @@
         parts = (high, (value - high.astype(F32)).astype(BF16))
         return jnp.concatenate([parts[k] for k in order], axis=axis)
 
-    is_owner = functools.reduce(jnp.logical_or, [me == place for place in places])
     slot = (me - first) // stride
 
     @pl.when(is_owner)
@@ -364,10 +391,10 @@
         offset = lax.broadcasted_iota(jnp.int32, (own, win_cols), 1) - win_cols // 2
         row_waves, col_waves = [], []
         for t in range(tilts):
-            waves = jnp.concatenate(wave(freq * (center_ref[t, 0] + step)), axis=0)
-            row_waves.append(thirds(waves, 1, (0, 0, 1)))
+            cos, sin = wave(freq * (center_ref[t, 0] + step))
+            row_waves.append(thirds(jnp.concatenate([cos, -sin], axis=1), 1, (0, 0, 1)))
             cos, sin = wave(cols * (center_ref[t, 1] + offset))
-            col_waves.append(thirds(jnp.concatenate([cos, -sin], axis=0), 0, (0, 1, 0)))
+            col_waves.append(halves(jnp.concatenate([cos, -sin], axis=0)))
         spot = lax.broadcasted_iota(jnp.int32, (own, band), 1)
         lower, start, middle = spot < half, spot == 0, spot == half
         ref_in[me, refs] = ref_out[slot]
@@ -415,15 +442,16 @@
             cross_re = spec_re * ref_re + spec_im * ref_im
             cross_im = spec_im * ref_re - spec_re * ref_im
             put_power(spec_re, spec_im, t)
-            turned = along(
-                row_waves[t],
-                thirds(jnp.concatenate([cross_re, cross_im], axis=0), 1, (0, 1, 0)),
-            )
-            moved_re = turned[:n, :own] - turned[n:, own:]
-            moved_im = turned[:n, own:] + turned[n:, :own]
-            part_out[t * n : (t + 1) * n, :] = jnp.dot(
-                thirds(jnp.concatenate([moved_re, moved_im], axis=1), 1, (0, 0, 1)),
-                col_waves[t], preferred_element_type=F32,
+            cross = jnp.concatenate([
+                jnp.concatenate([cross_re, cross_im], axis=1),
+                jnp.concatenate([cross_im, -cross_re], axis=1),
+            ], axis=0)
+            high, low = halves(along(row_waves[t], thirds(cross, 1, (0, 1, 0))))
+            near, far = col_waves[t]
+            part_out[t * n : (t + 1) * n, :] = (
+                jnp.dot(high, near, preferred_element_type=F32)
+                + jnp.dot(high, far, preferred_element_type=F32)
+                + jnp.dot(low, near, preferred_element_type=F32)
             )
         for d in range(n):
             @pl.when(me != d)
@@ -533,7 +561,7 @@
             pltpu.VMEM((tilts, n // 2) + message, F32),
             pltpu.VMEM(part, F32),
             pltpu.VMEM((owners,) + part, F32),
-            dma((9 + planes,)),
+            dma((9 + HALVES,)),
             dma, dma, dma((pairs,)), dma((pairs, PIECES)), dma((pairs,)), dma((pairs,)),
             dma((pairs,)), dma((tilts,)), dma, dma,
         ],

time: 21.4 us -> 20.8 us (0.972)
  Pallas kernels: 20.6 us -> 19.9 us
    pallas_call x1, Pallas kernels: 20 us -> 19.4 us  [run(): pl.pallas_call(functools.partial(fused_kernel, n, owners), out_shape=pltp...]
where the time goes in v3:
time: 20.8 us; the launch traced here: 20.6 us
  Pallas kernels  19.9 us (96%)
  between operations  0.64 us (3%)
    pallas_call x1, Pallas kernels, run(): pl.pallas_call(functools.partial(fused_kernel, n, owners), out_shape=pltp...  19.4 us
    pallas_call x1, Pallas kernels, run(): pl.pallas_call(finish_kernel, out_shape=(jax.ShapeDtypeStruct((tilts, 1,...  0.57 us

profile of v3, /device:TPU:0, one launch (start us, length us, event | category | flops | bytes accessed | tf_op | source)
XLA Modules:
  0.0 20.6 jit_solution(1990489734582234239)
XLA Ops:
  0.6 19.4 %fused.1.both_ref = f32[3,1,128]{2,1,0:T(1,128)S(1)} custom-call(s32[2,2]{1,0:T(2,128)} %center_hbm.1, s32[16]{0:T(128)} %owner_hbm.1, s32[2,2]{1,0:T(2,128)} %shift_hbm.1, f32[2,2]{1,0:T(2,128)} %weight_hbm.1, s32[2,1024]{1,0:T(2,128)} %left_ref.1, f32[2,1024]{1,0:T(2,128)} %share_ref.1, f32[1,2,128,128]{3,2,1,0:T(8,128)} %mine_ref.1, ...), custom_call_target="tpu_custom_call" | custom-call | tf_op jit(solution)/shard_map/fused/pallas_call | solution.py:528
  20.0 0.6 %finish.1 = (f32[2,1,128]{2,1,0:T(1,128)}, f32[2]{0:T(128)}) custom-call(f32[3,1,128]{2,1,0:T(1,128)S(1)} %fused.1.both_ref), custom_call_target="tpu_custom_call" | custom-call | tf_op jit(solution)/shard_map/finish/pallas_call | solution.py:577

commit v4 on v3

--- a/solution.py
+++ b/solution.py
@@ -15,7 +15,8 @@
 CHUNK = 256
 OWNERS = 4
 PIECES = 8
-HALVES = 2
+STOPS = (4, 8)
+PARTS = (3, 4)
 BF16 = jnp.bfloat16
 F32 = jnp.float32
 
@@ -57,7 +58,7 @@
     n, owners, center_hbm, owner_hbm, shift_hbm, weight_hbm,
     left_ref, share_ref, mine_ref, volume_ref, rowt_ref, colt_ref, out_ref,
     center_ref, owner_ref, shift_ref, weight_ref, left, share, mine, vol, rowt, colt,
-    onehot, shares, rows, extra, line, summed, give, take, stack, proj,
+    onehot, shares, rows, extra, line, summed, sofar, give, take, stack, proj,
     perm, line_keep, line_give, line_take, ref_out, ref_in, spec_out, spec_in, part_out, part_in,
     sems, ref_send, ref_recv, sib_send, sib_recv, line_send, line_recv,
     spec_send, spec_recv, part_send, part_recv,
@@ -91,6 +92,36 @@
             barrier, inc=1, device_id={"slab": device}, device_id_type=MESH
         )
 
+    def wait_entry():
+        others = owners + jnp.where(beside, 0, 1)
+        pl.semaphore_wait(barrier, jnp.where(is_owner, n - 1, others))
+
+    def local(source, into, k):
+        copy = pltpu.make_async_copy(source, into, sems.at[k])
+        copy.start()
+        return copy
+
+    ends = [chunks * part // 4 for part in PARTS]
+    begins = [0] + ends[:-1]
+
+    def columns_of(h):
+        return pl.ds(begins[h] * CHUNK, (ends[h] - begins[h]) * CHUNK)
+
+    get_left = local(left_ref, left, 0)
+    get_share = local(share_ref, share, 1)
+    get_table = local(rowt_ref, rowt, 6)
+    for h in range(len(PARTS)):
+        for z in range(planes):
+            for c in range(chunks):
+                part = (z, pl.ds(c * (height // chunks), height // chunks), columns_of(h))
+                local(volume_ref.at[part], vol.at[part], 9 + h)
+    scalars = [
+        local(shift_hbm, shift_ref, 2), local(weight_hbm, weight_ref, 3),
+        local(center_hbm, center_ref, 4), local(owner_hbm, owner_ref, 5),
+    ]
+    get_mine = local(mine_ref, mine, 7)
+    get_colt = local(colt_ref, colt, 8)
+
     @pl.when(is_owner)
     def _():
         for k in range(1, n):
@@ -101,33 +132,6 @@
         for place in places:
             greet(place)
         pl.when(jnp.logical_not(beside))(lambda: greet(sibling))
-
-    def wait_entry():
-        others = owners + jnp.where(beside, 0, 1)
-        pl.semaphore_wait(barrier, jnp.where(is_owner, n - 1, others))
-
-    def local(source, into, k):
-        copy = pltpu.make_async_copy(source, into, sems.at[k])
-        copy.start()
-        return copy
-
-    def columns_of(h):
-        return pl.ds(h * (width // HALVES), width // HALVES)
-
-    get_left = local(left_ref, left, 0)
-    get_share = local(share_ref, share, 1)
-    scalars = [
-        local(shift_hbm, shift_ref, 2), local(weight_hbm, weight_ref, 3),
-        local(center_hbm, center_ref, 4), local(owner_hbm, owner_ref, 5),
-    ]
-    get_table = local(rowt_ref, rowt, 6)
-    for h in range(HALVES):
-        for z in range(planes):
-            for c in range(chunks):
-                part = (z, pl.ds(c * (height // chunks), height // chunks), columns_of(h))
-                local(volume_ref.at[part], vol.at[part], 9 + h)
-    get_mine = local(mine_ref, mine, 7)
-    get_colt = local(colt_ref, colt, 8)
 
     def remote(source, into, send, recv, device):
         return pltpu.make_async_remote_copy(
@@ -232,7 +236,7 @@
         )
 
     def to_others(make):
-        for w in range(owners):
+        for w in reversed(range(owners)):
             pl.when(me != places[w])(lambda: make(w).start())
 
     refs = pl.ds(0, 2 * own)
@@ -287,30 +291,32 @@
             line_give[i, k : k + 1, :] = value[1:2, here]
         line_copy(i).start()
 
-    def merge(i):
-        def near(b):
-            here = slice(b * LANES, (b + 1) * LANES)
-            begin = (b * LANES) % span
-            total = summed[here, :] + take[i, b * LANES // span, begin : begin + LANES, :]
-            summed[here, :] = total
-            high, low = halves(total)
-            stack[here, 0:LANES] = high
-            stack[here, LANES : 2 * LANES] = low
-
-        def far(b):
-            here = slice(b * LANES, (b + 1) * LANES)
-            high, low = halves(summed[b * LANES + 1 : (b + 1) * LANES + 1, :])
-            stack[here, 2 * LANES : 3 * LANES] = high
-            stack[here, 3 * LANES :] = low
-
-        each = span // LANES
-        for k in range(pieces):
-            to_sibling(i, k).wait_recv()
-            for b in range(k * each, (k + 1) * each):
-                near(b)
-                if b:
-                    far(b - 1)
-        far(blocks - 1)
+    each = span // LANES
+
+    def near(i, b):
+        here = slice(b * LANES, (b + 1) * LANES)
+        if b % each == 0:
+            to_sibling(i, b // each).wait_recv()
+        begin = (b % each) * LANES
+        total = summed[here, :] + take[i, b // each, begin : begin + LANES, :]
+        summed[here, :] = total
+        high, low = halves(total)
+        stack[here, 0:LANES] = high
+        stack[here, LANES : 2 * LANES] = low
+
+    def far(b):
+        here = slice(b * LANES, (b + 1) * LANES)
+        high, low = halves(summed[b * LANES + 1 : (b + 1) * LANES + 1, :])
+        stack[here, 2 * LANES : 3 * LANES] = high
+        stack[here, 3 * LANES :] = low
+
+    def merge(i, begin, end):
+        for b in range(begin + (1 if begin else 0), min(end + 1, blocks)):
+            near(i, b)
+            if b > begin:
+                far(b - 1)
+        if end == blocks:
+            far(blocks - 1)
 
     def put_line(i):
         line_copy(i).wait_recv()
@@ -323,16 +329,23 @@
                 block = pltpu.roll(jnp.broadcast_to(block, (SUBLANES, LANES)), LANES - offset, 1)
             spec_out[i, w, 2 * own : 2 * own + 1, :] = block[0:1]
 
-    def gather(i):
+    def gather(i, begin, end):
+        deep = slice(begin * LANES, end * LANES)
         for c in range(chunks):
             here = slice(c * CHUNK, (c + 1) * CHUNK)
-            picked = jnp.dot(onehot[i, here, :], stack[...], preferred_element_type=F32)
+            picked = jnp.dot(onehot[i, here, deep], stack[deep, :], preferred_element_type=F32)
             near = picked[:, :LANES] + picked[:, LANES : 2 * LANES]
             far = picked[:, 2 * LANES : 3 * LANES] + picked[:, 3 * LANES :]
             part = shares[i, here, :]
-            high, low = halves((1.0 - part) * near + part * far)
-            proj[here, :LANES] = high
-            proj[here, LANES:] = low
+            value = (1.0 - part) * near + part * far
+            if begin:
+                value = value + sofar[here, :]
+            if end < blocks:
+                sofar[here, :] = value
+            else:
+                high, low = halves(value)
+                proj[here, :LANES] = high
+                proj[here, LANES:] = low
 
     def columns(i):
         both = jnp.dot(colt[...], proj[...], preferred_element_type=F32)
@@ -345,15 +358,15 @@
     for copy in scalars:
         copy.wait()
     sent = 0
-    for h in range(HALVES):
+    for h in range(len(PARTS)):
         part = (slice(None), slice(None), columns_of(h))
         pltpu.make_async_copy(volume_ref.at[part], vol.at[part], sems.at[9 + h]).wait()
         for z in range(planes):
-            for c in range(chunks // HALVES):
-                row_chunk(z, h * (chunks // HALVES) + c)
+            for c in range(begins[h], ends[h]):
+                row_chunk(z, c)
         if h == 0:
             wait_entry()
-        known = (h + 1) * (width // HALVES)
+        known = ends[h] * CHUNK
         ready = pieces if known == width else (known - pad) // span
         for k in range(sent, ready):
             give_piece(k)
@@ -365,8 +378,10 @@
         last_line(i)
     for i in range(pairs):
         own_part(i)
-        merge(i)
-        gather(i)
+        stops = [blocks * stop // 8 for stop in STOPS]
+        for begin, end in zip([0] + stops[:-1], stops):
+            merge(i, begin, end)
+            gather(i, begin, end)
         columns(i)
         put_line(i)
         to_others(functools.partial(to_owner, i))
@@ -417,7 +432,6 @@
                 remote_count -= 1
             arrived = spec_in.at[t, pl.ds(0, remote_count), used]
             remote(arrived, arrived, spec_send.at[0], spec_recv.at[t], me).wait_recv()
-        for t in range(tilts):
             total = spec_in[t, 0, : 2 * own]
             last = spec_in[t, 0, 2 * own : 2 * own + 1]
             for e in range(1, n // 2):
@@ -547,6 +561,7 @@
             pltpu.VMEM((planes, blocks, LANES), F32),
             pltpu.VMEM((SUBLANES, width), F32),
             pltpu.VMEM((width + SUBLANES, LANES), F32),
+            pltpu.VMEM((width, LANES), F32),
             pltpu.VMEM((pairs, PIECES, width // PIECES, LANES), F32),
             pltpu.VMEM((pairs, PIECES, width // PIECES, LANES), F32),
             pltpu.VMEM((width, 4 * LANES), BF16),
@@ -561,7 +576,7 @@
             pltpu.VMEM((tilts, n // 2) + message, F32),
             pltpu.VMEM(part, F32),
             pltpu.VMEM((owners,) + part, F32),
-            dma((9 + HALVES,)),
+            dma((9 + len(PARTS),)),
             dma, dma, dma((pairs,)), dma((pairs, PIECES)), dma((pairs,)), dma((pairs,)),
             dma((pairs,)), dma((tilts,)), dma, dma,
         ],

time: 20.8 us -> 20.4 us (0.981)
  Pallas kernels: 19.9 us -> 19.6 us
    pallas_call x1, Pallas kernels: 19.4 us -> 19 us  [run(): pl.pallas_call(functools.partial(fused_kernel, n, owners), out_shape=pltp...]
where the time goes in v4:
time: 20.4 us; the launch traced here: 20.2 us
  Pallas kernels  19.6 us (96%)
  between operations  0.64 us (3%)
    pallas_call x1, Pallas kernels, run(): pl.pallas_call(functools.partial(fused_kernel, n, owners), out_shape=pltp...  19 us
    pallas_call x1, Pallas kernels, run(): pl.pallas_call(finish_kernel, out_shape=(jax.ShapeDtypeStruct((tilts, 1,...  0.57 us

profile of v4, /device:TPU:0, one launch (start us, length us, event | category | flops | bytes accessed | tf_op | source)
XLA Modules:
  0.0 20.2 jit_solution(3569140958570106721)
XLA Ops:
  0.6 19.0 %fused.1.both_ref = f32[3,1,128]{2,1,0:T(1,128)S(1)} custom-call(s32[2,2]{1,0:T(2,128)} %center_hbm.1, s32[16]{0:T(128)} %owner_hbm.1, s32[2,2]{1,0:T(2,128)} %shift_hbm.1, f32[2,2]{1,0:T(2,128)} %weight_hbm.1, s32[2,1024]{1,0:T(2,128)} %left_ref.1, f32[2,1024]{1,0:T(2,128)} %share_ref.1, f32[1,2,128,128]{3,2,1,0:T(8,128)} %mine_ref.1, ...), custom_call_target="tpu_custom_call" | custom-call | tf_op jit(solution)/shard_map/fused/pallas_call | solution.py:542
  19.6 0.6 %finish.1 = (f32[2,1,128]{2,1,0:T(1,128)}, f32[2]{0:T(128)}) custom-call(f32[3,1,128]{2,1,0:T(1,128)S(1)} %fused.1.both_ref), custom_call_target="tpu_custom_call" | custom-call | tf_op jit(solution)/shard_map/finish/pallas_call | solution.py:592

commit v5 on v4

--- a/solution.py
+++ b/solution.py
@@ -112,8 +112,8 @@
     get_table = local(rowt_ref, rowt, 6)
     for h in range(len(PARTS)):
         for z in range(planes):
-            for c in range(chunks):
-                part = (z, pl.ds(c * (height // chunks), height // chunks), columns_of(h))
+            for c in range(2):
+                part = (z, pl.ds(c * (height // 2), height // 2), columns_of(h))
                 local(volume_ref.at[part], vol.at[part], 9 + h)
     scalars = [
         local(shift_hbm, shift_ref, 2), local(weight_hbm, weight_ref, 3),

time: 20.4 us -> 20.4 us (level)
  no operation moved by 1% of the time
where the time goes in v5:
time: 20.4 us; the launch traced here: 20.3 us
  Pallas kernels  19.6 us (96%)
  between operations  0.64 us (3%)
    pallas_call x1, Pallas kernels, run(): pl.pallas_call(functools.partial(fused_kernel, n, owners), out_shape=pltp...  19.1 us
    pallas_call x1, Pallas kernels, run(): pl.pallas_call(finish_kernel, out_shape=(jax.ShapeDtypeStruct((tilts, 1,...  0.57 us

profile of v5, /device:TPU:0, one launch (start us, length us, event | category | flops | bytes accessed | tf_op | source)
XLA Modules:
  0.0 20.3 jit_solution(11675407142543599797)
XLA Ops:
  0.6 19.1 %fused.1.both_ref = f32[3,1,128]{2,1,0:T(1,128)S(1)} custom-call(s32[2,2]{1,0:T(2,128)} %center_hbm.1, s32[16]{0:T(128)} %owner_hbm.1, s32[2,2]{1,0:T(2,128)} %shift_hbm.1, f32[2,2]{1,0:T(2,128)} %weight_hbm.1, s32[2,1024]{1,0:T(2,128)} %left_ref.1, f32[2,1024]{1,0:T(2,128)} %share_ref.1, f32[1,2,128,128]{3,2,1,0:T(8,128)} %mine_ref.1, ...), custom_call_target="tpu_custom_call" | custom-call | tf_op jit(solution)/shard_map/fused/pallas_call | solution.py:542
  19.7 0.6 %finish.1 = (f32[2,1,128]{2,1,0:T(1,128)}, f32[2]{0:T(128)}) custom-call(f32[3,1,128]{2,1,0:T(1,128)S(1)} %fused.1.both_ref), custom_call_target="tpu_custom_call" | custom-call | tf_op jit(solution)/shard_map/finish/pallas_call | solution.py:592
